TPU v7x, 32 devices: a whole 2x2x4 slice. The times are simulated.
32 devices in a mesh: gx: 8 (over y, x, core), gy: 4 (over z).
Axes of the slice: x: 2, y: 2, z: 4, core: 2. Of those that a mesh axis runs over, the one named last changes fastest.
Arguments:
- volts: float32 [32, 4, 64, 512], P(None, None, 'gx', 'gy'), may hold values from -6 to 6
- cap: float32 [4, 64, 512], P(None, 'gx', 'gy'), may hold values from 0.05 to 1
- cond_x: float32 [4, 64, 512], P(None, 'gx', 'gy'), may hold values from 0.5 to 2
- cond_y: float32 [4, 64, 512], P(None, 'gx', 'gy'), may hold values from 0.5 to 2
- via: float32 [4, 64, 512], P(None, 'gx', 'gy'), may hold values from 0.2 to 2
- waveforms: float32 [64, 64], replicated, may hold values from -6 to 6
- placement: int32 [262144, 1], P(('gx', 'gy')), may hold values from 0 to 31; in each aligned block of 8192 rows (0 to 8191, 8192 to 16383, ...) at most 512 rows name the same one
- cells: int32 [262144], P(('gx', 'gy')), may hold values from 0 to 1023
- wave_ids: int32 [262144], P(('gx', 'gy')), may hold values from 0 to 63
- amps: float32 [262144], P(('gx', 'gy')), may hold values from 0.5 to 4
Outputs:
- volts_out: float32 [32, 4, 64, 512], P(None, None, 'gx', 'gy')
- residual: float32 [32, 4, 64, 512], P(None, None, 'gx', 'gy')
Inputs may be any that keep to these rules, and one draw needn't show every extreme that they name: `placement`: in each device's block of 8192 rows no tile is named more than 512 times, a bound that some block reaches.
All inputs are finite; a program needn't handle non-finite values.
Results may differ from a plain program's by a relative error of at most 0.0029.
Values may be sent and summed in bfloat16 or wider, within the bound.
A program may use at most 64 MiB of HBM per device.

v0:
```python
import jax
import jax.numpy as jnp
from jax import lax
from jax.sharding import PartitionSpec as P

ITERS = 3


def with_halo(block, sides, width):
    for axis, dim in sides:
        count = lax.axis_size(axis)
        forward = [(i, i + 1) for i in range(count - 1)]
        backward = [(target, source) for source, target in forward]
        low = lax.ppermute(
            lax.slice_in_dim(block, block.shape[dim] - width, None, axis=dim), axis, forward
        )
        high = lax.ppermute(lax.slice_in_dim(block, 0, width, axis=dim), axis, backward)
        block = jnp.concatenate([low, block, high], axis=dim)
    return block


def shifted(x, axis, by):
    length = lax.axis_size(axis)
    pairs = [(i, i + by) for i in range(length) if 0 <= i + by < length]
    return lax.ppermute(x, axis, pairs)


def gram(left, right):
    left_rows = left.reshape(left.shape[0], -1)
    right_rows = right.reshape(right.shape[0], -1)
    return lax.dot_general(
        left_rows, right_rows, (((1,), (1,)), ((), ())), precision=lax.Precision.HIGHEST
    )


def combine(coef, field):
    return jnp.einsum("st,slxy->tlxy", coef, field, precision=lax.Precision.HIGHEST)


def spd_solve(matrix, right):
    factor = jnp.linalg.cholesky(matrix)
    return jax.scipy.linalg.cho_solve((factor, True), right)


def make_currents(waveforms, kinds, scales):
    table_hits = (
        jnp.arange(waveforms.shape[1], dtype=jnp.int32)[:, None] == kinds[None, :]
    ).astype(jnp.float32)
    picked = jnp.dot(waveforms, table_hits, precision=lax.Precision.HIGHEST)
    return (picked * scales[None, :]).astype(jnp.bfloat16)


def operate(field, cap, cond_x, cond_x_low, cond_y, cond_y_low, via, via_low):
    padded = with_halo(field, (("gx", 2), ("gy", 3)), 1)
    zero_layer = jnp.zeros_like(field[:, :1])
    upper = jnp.concatenate([field[:, 1:], zero_layer], axis=1)
    lower = jnp.concatenate([zero_layer, field[:, :-1]], axis=1)
    result = cap * field
    result = result + cond_x * (field - padded[:, :, 2:, 1:-1])
    result = result + cond_x_low * (field - padded[:, :, :-2, 1:-1])
    result = result + cond_y * (field - padded[:, :, 1:-1, 2:])
    result = result + cond_y_low * (field - padded[:, :, 1:-1, :-2])
    result = result + via * (field - upper) + via_low * (field - lower)
    return result


def body(volts, cap, cond_x, cond_y, via, waveforms, placement, cells, wave_ids, amps):
    devices = lax.axis_size(("gx", "gy"))
    scenarios = volts.shape[0]
    steps = waveforms.shape[0] // scenarios
    tile_x = volts.shape[2]
    tile_y = volts.shape[3]
    die_cells = tile_x * tile_y
    slots_all = 2 * cells.shape[0]
    capacity = slots_all // devices
    target = placement[:, 0]
    target_hits = (jnp.arange(devices, dtype=jnp.int32)[:, None] == target[None, :]).astype(
        jnp.int32
    )
    running = jnp.cumsum(target_hits, axis=1) - 1
    position = jnp.sum(target_hits * running, axis=0)
    slot_index = target * capacity + position
    currents = make_currents(waveforms, wave_ids, amps)
    packed = jnp.zeros((currents.shape[0], slots_all), jnp.bfloat16).at[:, slot_index].set(currents)
    cell_slots = jnp.zeros((1, slots_all), jnp.int32).at[0, slot_index].set(cells)
    arrived, cell_slots = (
        lax.all_to_all(packed, ("gx", "gy"), split_axis=1, concat_axis=1, tiled=True),
        lax.all_to_all(cell_slots, ("gx", "gy"), split_axis=1, concat_axis=1, tiled=True),
    )
    block_rows = min(1024, slots_all)
    block_count = slots_all // block_rows
    cell_line = jnp.arange(die_cells, dtype=jnp.int32)

    def add_block(turn, total):
        piece_values = lax.dynamic_slice_in_dim(arrived, turn * block_rows, block_rows, 1)
        piece_cells = lax.dynamic_slice_in_dim(cell_slots[0], turn * block_rows, block_rows, 0)
        one_hot = (piece_cells[:, None] == cell_line[None, :]).astype(jnp.bfloat16)
        return total + jnp.dot(piece_values, one_hot, preferred_element_type=jnp.float32)

    injected = lax.fori_loop(
        0, block_count, add_block, jnp.zeros((arrived.shape[0], die_cells), jnp.float32)
    )
    injected = injected.reshape(steps, scenarios, tile_x, tile_y)
    rim_x = shifted(cond_x[:, -1:, :], "gx", 1)
    rim_y = shifted(cond_y[:, :, -1:], "gy", 1)
    cond_x_low = jnp.concatenate([rim_x, cond_x[:, :-1, :]], axis=1)
    cond_y_low = jnp.concatenate([rim_y, cond_y[:, :, :-1]], axis=2)
    via_low = jnp.concatenate([jnp.zeros_like(via[:1]), via[:-1]], axis=0)

    def apply_grid(field):
        return operate(field, cap, cond_x, cond_x_low, cond_y, cond_y_low, via, via_low)

    voltage = volts
    residual = volts
    for step in range(steps):
        rhs = cap * voltage
        rhs = rhs.at[:, 0].add(-injected[step])
        iterate = voltage
        residual = rhs - apply_grid(iterate)
        direction = residual
        norm_gram = lax.psum(gram(residual, residual), ("gx", "gy"))
        for sweep in range(ITERS):
            image = apply_grid(direction)
            curve_gram, cross_gram, image_gram = lax.psum(
                (gram(direction, image), gram(residual, image), gram(image, image)), ("gx", "gy")
            )
            step_coef = spd_solve(curve_gram, norm_gram)
            iterate = iterate + combine(step_coef, direction)
            residual = residual - combine(step_coef, image)
            if sweep + 1 < ITERS:
                cross_term = jnp.dot(cross_gram, step_coef, precision=lax.Precision.HIGHEST)
                square_term = jnp.dot(
                    step_coef.T,
                    jnp.dot(image_gram, step_coef, precision=lax.Precision.HIGHEST),
                    precision=lax.Precision.HIGHEST,
                )
                new_gram = norm_gram - cross_term - cross_term.T + square_term
                turn_coef = spd_solve(norm_gram, new_gram)
                direction = residual + combine(turn_coef, direction)
                norm_gram = new_gram
        voltage = iterate
    return (voltage, residual)


def solution(mesh):
    return jax.shard_map(
        body,
        mesh=mesh,
        in_specs=(
            P(None, None, "gx", "gy"),
            P(None, "gx", "gy"),
            P(None, "gx", "gy"),
            P(None, "gx", "gy"),
            P(None, "gx", "gy"),
            P(),
            P(("gx", "gy"), None),
            P(("gx", "gy")),
            P(("gx", "gy")),
            P(("gx", "gy")),
        ),
        out_specs=(P(None, None, "gx", "gy"), P(None, None, "gx", "gy")),
        check_vma=False,
    )
```

profile of v0, /device:TPU:0, one launch (start us, length us, event | category | flops | bytes accessed | tf_op | source)
XLA Modules:
  0.0 647.4 jit_solution(1546838298687216187)
XLA Ops:
  1.6 9.5 %reduce-window.6 = s32[32,64,128]{2,1,0:T(8,128)S(1)} reduce-window(s32[32,64,128]{2,1,0:T(8,128)S(1)} %fusion.11, s32[]{:T(128)} %constant.128.clone.1), window={size=1x1x128 pad=0_0x0_0x127_0}, to_apply=%region_0.0 | reduce-window | flops 33292288 | bytes 2097156 | tf_op jit(solution)/shard_map/reduce-window
  14.9 23.7 %scatter_custom_fusion = bf16[64,16384]{0,1:T(8,128)(2,1)} fusion(s32[8192]{0:T(1024)S(1)} %bitcast.343, bf16[8192,64]{1,0:T(8,128)(2,1)S(1)} %copy.219, bf16[]{:T(256)} %constant.130.clone.1), kind=kCustom, calls=%fused_computation.13 | custom fusion | bytes 2097154 | tf_op jit(solution)/shard_map/scatter | solution.py:84
  38.6 4.8 copy.220
  43.3 7.3 %all-to-all-start = ((bf16[64,32,512]{2,0,1:T(8,128)(2,1)}), bf16[64,32,512]{2,0,1:T(8,128)(2,1)S(1)}, u32[]{:S(2)}, u32[]{:S(2)}) async-start(bf16[64,32,512]{2,0,1:T(8,128)(2,1)} %copy.220), calls=%async_computation | async-start | bytes 4194304 | tf_op jit(solution)/shard_map/all_to_all | solution.py:87
  55.2 3.5 collective-permute-start.4
  58.8 3.7 collective-permute-start.1
  62.9 31.2 %scatter_custom_fusion.1 = s32[16384]{0:T(1024)} fusion(s32[8192]{0:T(1024)S(1)} %broadcast_select_fusion, s32[8192]{0:T(1024)} %param.26, s32[]{:T(128)} %constant.128.clone.1), kind=kCustom, calls=%fused_computation.270 | custom fusion | bytes 66048
  97.6 7.3 %all-to-all-start.1 = ((s32[1,32,512]{2,0,1:T(1,128)}), s32[1,32,512]{2,0,1:T(1,128)}, u32[]{:S(2)}, u32[]{:S(2)}) async-start(s32[1,32,512]{2,0,1:T(1,128)} %bitcast.344), calls=%async_computation.1 | async-start | bytes 131072 | tf_op jit(solution)/shard_map/all_to_all | solution.py:88
  110.3 4.7 collective-permute-start.5
  119.0 53.7 %while.16 = (s32[]{:T(128)}, f32[64,1024]{1,0:T(8,128)}, bf16[64,16384]{1,0:T(8,128)(2,1)}, s32[1,16384]{1,0:T(1,128)}, s32[]{:T(128)}, /*index=5*/s32[]{:T(128)}, s32[]{:T(128)}, s32[]{:T(128)}) while((s32[]{:T(128)}, f32[64,1024]{1,0:T(8,128)}, bf16[64,16384]{1,0:T(8,128)(2,1)}, s32[1,16384]{1,0:T(1,128)}, s32[]{:T(128)}, ...), condition=%wide.region_6.7_spmd.clone, body=%wide.region_5.6_spmd.clone.sunk | while | flops 135397376 | bytes 667797 | solution.py:100
  183.8 4.8 collective-permute-start.9
  192.3 44.5 %all-reduce.21 = (f32[32,32]{0,1:T(8,128)S(1)}, f32[32,32]{0,1:T(8,128)S(1)}, f32[32,32]{1,0:T(8,128)S(1)}) all-reduce(f32[32,32]{0,1:T(8,128)S(1)} %convolution_bitcast_fusion.18, f32[32,32]{0,1:T(8,128)S(1)} %convolution_bitcast_fusion.19, f32[32,32]{1,0:T(8,128)S(1)} %convolution_bitcast_fusion.17), channel_id=1, replica_groups=mesh['gx'=8,'gy'=4] {'gx','gy'}, use_global_device_ids=true, to_apply=%region_10.12 | all-reduce | flops 3072 | bytes 24576 | tf_op jit(solution)/shard_map/psum | solution.py:121
  266.5 4.8 collective-permute-start.13
  279.1 43.3 %all-reduce.20 = (f32[32,32]{0,1:T(8,128)S(1)}, f32[32,32]{1,0:T(8,128)S(1)}, f32[32,32]{1,0:T(8,128)S(1)}) all-reduce(f32[32,32]{0,1:T(8,128)S(1)} %convolution_bitcast_fusion.15, f32[32,32]{1,0:T(8,128)S(1)} %convolution_bitcast_fusion.13, f32[32,32]{1,0:T(8,128)S(1)} %convolution_bitcast_fusion.14), channel_id=1, replica_groups=mesh['gx'=8,'gy'=4] {'gx','gy'}, use_global_device_ids=true, to_apply=%region_12.15 | all-reduce | flops 3072 | bytes 24576 | tf_op jit(solution)/shard_map/psum | solution.py:124
  340.4 4.5 collective-permute-start.17
  347.8 43.9 %psum.110 = f32[32,32]{0,1:T(8,128)S(1)} all-reduce(f32[32,32]{0,1:T(8,128)S(1)} %convolution_bitcast_fusion.11), channel_id=1, replica_groups=mesh['gx'=8,'gy'=4] {'gx','gy'}, use_global_device_ids=true, to_apply=%region_15.18 | all-reduce | flops 1024 | bytes 8192 | tf_op jit(solution)/shard_map/psum | solution.py:124
  408.1 5.0 collective-permute-start.21
  417.5 3.3 collective-permute-start.23
  425.1 4.6 collective-permute-start.25
  434.3 46.8 %all-reduce.19 = (f32[32,32]{0,1:T(8,128)S(1)}, f32[32,32]{0,1:T(8,128)S(1)}, f32[32,32]{1,0:T(8,128)S(1)}) all-reduce(f32[32,32]{0,1:T(8,128)S(1)} %convolution_bitcast_fusion.8, f32[32,32]{0,1:T(8,128)S(1)} %convolution_bitcast_fusion.9, f32[32,32]{1,0:T(8,128)S(1)} %convolution_bitcast_fusion.7), channel_id=1, replica_groups=mesh['gx'=8,'gy'=4] {'gx','gy'}, use_global_device_ids=true, to_apply=%region_17.20 | all-reduce | flops 3072 | bytes 24576 | tf_op jit(solution)/shard_map/psum | solution.py:121
  510.3 4.7 collective-permute-start.29
  522.7 42.7 %all-reduce.18 = (f32[32,32]{0,1:T(8,128)S(1)}, f32[32,32]{1,0:T(8,128)S(1)}, f32[32,32]{1,0:T(8,128)S(1)}) all-reduce(f32[32,32]{0,1:T(8,128)S(1)} %convolution_bitcast_fusion.5, f32[32,32]{1,0:T(8,128)S(1)} %convolution_bitcast_fusion.3, f32[32,32]{1,0:T(8,128)S(1)} %convolution_bitcast_fusion.4), channel_id=1, replica_groups=mesh['gx'=8,'gy'=4] {'gx','gy'}, use_global_device_ids=true, to_apply=%region_19.22 | all-reduce | flops 3072 | bytes 24576 | tf_op jit(solution)/shard_map/psum | solution.py:124
  583.3 4.5 collective-permute-start.33
  592.0 44.5 %psum.117 = f32[32,32]{0,1:T(8,128)S(1)} all-reduce(f32[32,32]{0,1:T(8,128)S(1)} %convolution_bitcast_fusion.1), channel_id=1, replica_groups=mesh['gx'=8,'gy'=4] {'gx','gy'}, use_global_device_ids=true, to_apply=%region_22.25 | all-reduce | flops 1024 | bytes 8192 | tf_op jit(solution)/shard_map/psum | solution.py:124
  (397 shorter events, 247.3 us)
Async XLA Ops:
  43.3 54.2 %all-to-all-start = ((bf16[64,32,512]{2,0,1:T(8,128)(2,1)}), bf16[64,32,512]{2,0,1:T(8,128)(2,1)S(1)}, u32[]{:S(2)}, u32[]{:S(2)}) async-start(bf16[64,32,512]{2,0,1:T(8,128)(2,1)} %copy.220), calls=%async_computation | async-start | bytes 4194304 | tf_op jit(solution)/shard_map/all_to_all | solution.py:87
  51.7 43.5 %collective-permute-start.2 = (f32[32,4,1,128]{3,0,2,1:T(8,128)S(1)}, f32[32,4,1,128]{3,0,2,1:T(8,128)S(1)}, u32[]{:S(2)}, u32[]{:S(2)}) collective-permute-start(f32[32,4,1,128]{3,0,2,1:T(8,128)S(1)} %get-tuple-element.215), channel_id=1, source_target_pairs={{0,4},{4,8},{8,12},{12,16},{16,20},{20,24},{24,28},{1,5},{5,9},{9,... | collective-permute-start | bytes 196616 | tf_op jit(solution)/shard_map/ppermute | solution.py:14
  53.8 43.6 %collective-permute-start = (f32[32,4,1,128]{3,0,2,1:T(8,128)}, f32[32,4,1,128]{3,0,2,1:T(8,128)S(1)}, u32[]{:S(2)}, u32[]{:S(2)}) collective-permute-start(f32[32,4,1,128]{3,0,2,1:T(8,128)} %get-tuple-element.214), channel_id=1, source_target_pairs={{4,0},{8,4},{12,8},{16,12},{20,16},{24,20},{28,24},{5,1},{9,5},{13... | collective-permute-start | bytes 196616 | tf_op jit(solution)/shard_map/ppermute | solution.py:17
  55.2 39.9 %collective-permute-start.4 = (f32[4,8,1]{2,1,0:T(8,128)S(1)}, f32[4,8,1]{2,1,0:T(8,128)S(1)}, u32[]{:S(2)}, u32[]{:S(2)}) collective-permute-start(f32[4,8,1]{2,1,0:T(8,128)S(1)} %slice.379), channel_id=1, source_target_pairs={{0,1},{1,2},{2,3},{4,5},{5,6},{6,7},{8,9},{9,10},{10,11},{12,13},{... | collective-permute-start | bytes 392 | tf_op jit(solution)/shard_map/ppermute | solution.py:25
  58.8 56.2 %collective-permute-start.1 = (f32[4,1,128]{2,1,0:T(1,128)S(1)}, f32[4,1,128]{2,1,0:T(1,128)S(1)}, u32[]{:S(2)}, u32[]{:S(2)}) collective-permute-start(f32[4,1,128]{2,1,0:T(1,128)S(1)} %slice.373), channel_id=1, source_target_pairs={{0,4},{4,8},{8,12},{12,16},{16,20},{20,24},{24,28},{1,5},{5,9},{9,... | collective-permute-start | bytes 6152 | tf_op jit(solution)/shard_map/ppermute | solution.py:25
  97.6 21.4 %all-to-all-start.1 = ((s32[1,32,512]{2,0,1:T(1,128)}), s32[1,32,512]{2,0,1:T(1,128)}, u32[]{:S(2)}, u32[]{:S(2)}) async-start(s32[1,32,512]{2,0,1:T(1,128)} %bitcast.344), calls=%async_computation.1 | async-start | bytes 131072 | tf_op jit(solution)/shard_map/all_to_all | solution.py:88
  107.6 7.4 %collective-permute-start.3 = (f32[32,4,10,1]{0,1,3,2:T(4,128)S(1)}, f32[32,4,10,1]{0,1,3,2:T(4,128)S(1)}, u32[]{:S(2)}, u32[]{:S(2)}) collective-permute-start(f32[32,4,10,1]{0,1,3,2:T(4,128)S(1)} %copy.230), channel_id=1, source_target_pairs={{1,0},{2,1},{3,2},{5,4},{6,5},{7,6},{9,8},{10,9},{11,10},{13,12},{... | collective-permute-start | bytes 15368 | tf_op jit(solution)/shard_map/ppermute | solution.py:17
  110.3 6.0 collective-permute-start.5
  182.2 7.7 %collective-permute-start.8 = (f32[32,4,10,1]{0,1,3,2:T(4,128)S(1)}, f32[32,4,10,1]{0,1,3,2:T(4,128)S(1)}, u32[]{:S(2)}, u32[]{:S(2)}) collective-permute-start(f32[32,4,10,1]{0,1,3,2:T(4,128)S(1)} %copy.240), channel_id=1, source_target_pairs={{1,0},{2,1},{3,2},{5,4},{6,5},{7,6},{9,8},{10,9},{11,10},{13,12},{... | collective-permute-start | bytes 15368 | tf_op jit(solution)/shard_map/ppermute | solution.py:17
  183.8 6.4 collective-permute-start.9
  264.9 10.1 %collective-permute-start.12 = (f32[32,4,10,1]{0,1,3,2:T(4,128)S(1)}, f32[32,4,10,1]{0,1,3,2:T(4,128)S(1)}, u32[]{:S(2)}, u32[]{:S(2)}) collective-permute-start(f32[32,4,10,1]{0,1,3,2:T(4,128)S(1)} %copy.254), channel_id=1, source_target_pairs={{1,0},{2,1},{3,2},{5,4},{6,5},{7,6},{9,8},{10,9},{11,10},{13,12},{... | collective-permute-start | bytes 15368 | tf_op jit(solution)/shard_map/ppermute | solution.py:17
  266.5 8.9 %collective-permute-start.13 = (f32[32,4,10,1]{0,1,3,2:T(4,128)S(1)}, f32[32,4,10,1]{0,1,3,2:T(4,128)S(1)}, u32[]{:S(2)}, u32[]{:S(2)}) collective-permute-start(f32[32,4,10,1]{0,1,3,2:T(4,128)S(1)} %copy.256), channel_id=1, source_target_pairs={{0,1},{1,2},{2,3},{4,5},{5,6},{6,7},{8,9},{9,10},{10,11},{12,13},{... | collective-permute-start | bytes 15368 | tf_op jit(solution)/shard_map/ppermute | solution.py:14
  338.8 6.3 collective-permute-start.16
  340.4 6.0 collective-permute-start.17
  399.5 5.2 collective-permute-start.18
  406.5 6.6 %collective-permute-start.20 = (f32[32,4,10,1]{0,1,3,2:T(4,128)S(1)}, f32[32,4,10,1]{0,1,3,2:T(4,128)S(1)}, u32[]{:S(2)}, u32[]{:S(2)}) collective-permute-start(f32[32,4,10,1]{0,1,3,2:T(4,128)S(1)} %copy.274), channel_id=1, source_target_pairs={{1,0},{2,1},{3,2},{5,4},{6,5},{7,6},{9,8},{10,9},{11,10},{13,12},{... | collective-permute-start | bytes 15368 | tf_op jit(solution)/shard_map/ppermute | solution.py:17
  408.1 6.0 collective-permute-start.21
  416.2 5.4 collective-permute-start.22
  423.5 6.7 %collective-permute-start.24 = (f32[32,4,10,1]{0,1,3,2:T(4,128)S(1)}, f32[32,4,10,1]{0,1,3,2:T(4,128)S(1)}, u32[]{:S(2)}, u32[]{:S(2)}) collective-permute-start(f32[32,4,10,1]{0,1,3,2:T(4,128)S(1)} %copy.278), channel_id=1, source_target_pairs={{1,0},{2,1},{3,2},{5,4},{6,5},{7,6},{9,8},{10,9},{11,10},{13,12},{... | collective-permute-start | bytes 15368 | tf_op jit(solution)/shard_map/ppermute | solution.py:17
  425.1 6.0 collective-permute-start.25
  508.7 10.0 %collective-permute-start.28 = (f32[32,4,10,1]{0,1,3,2:T(4,128)S(1)}, f32[32,4,10,1]{0,1,3,2:T(4,128)S(1)}, u32[]{:S(2)}, u32[]{:S(2)}) collective-permute-start(f32[32,4,10,1]{0,1,3,2:T(4,128)S(1)} %copy.291), channel_id=1, source_target_pairs={{1,0},{2,1},{3,2},{5,4},{6,5},{7,6},{9,8},{10,9},{11,10},{13,12},{... | collective-permute-start | bytes 15368 | tf_op jit(solution)/shard_map/ppermute | solution.py:17
  510.3 8.8 %collective-permute-start.29 = (f32[32,4,10,1]{0,1,3,2:T(4,128)S(1)}, f32[32,4,10,1]{0,1,3,2:T(4,128)S(1)}, u32[]{:S(2)}, u32[]{:S(2)}) collective-permute-start(f32[32,4,10,1]{0,1,3,2:T(4,128)S(1)} %copy.293), channel_id=1, source_target_pairs={{0,1},{1,2},{2,3},{4,5},{5,6},{6,7},{8,9},{9,10},{10,11},{12,13},{... | collective-permute-start | bytes 15368 | tf_op jit(solution)/shard_map/ppermute | solution.py:14
  581.7 7.1 %collective-permute-start.32 = (f32[32,4,10,1]{0,1,3,2:T(4,128)S(1)}, f32[32,4,10,1]{0,1,3,2:T(4,128)S(1)}, u32[]{:S(2)}, u32[]{:S(2)}) collective-permute-start(f32[32,4,10,1]{0,1,3,2:T(4,128)S(1)} %copy.303), channel_id=1, source_target_pairs={{1,0},{2,1},{3,2},{5,4},{6,5},{7,6},{9,8},{10,9},{11,10},{13,12},{... | collective-permute-start | bytes 15368 | tf_op jit(solution)/shard_map/ppermute | solution.py:17
  583.3 6.0 collective-permute-start.33
  (49 other events, 728.9 us)
where the time goes:
time: 657 us; the launch traced here: 647 us
  blocking collectives  266 us (40%)
  local copies, waits for them, and re-layouts  107 us (16%)
  starting transfers between devices  104 us (16%)
  other arithmetic  95.1 us (14%)
  matrix products  68.5 us (10%)
    psum x4, blocking collectives, body(): lax.psum((gram(direction, image), gram(residual, image), gram(image, imag...  174 us
    psum x2, blocking collectives, body(): norm_gram = lax.psum(gram(residual, residual), ('gx', 'gy'))  91.3 us
    ppermute x16, starting transfers between devices, with_halo(): lax.ppermute(lax.slice_in_dim(block, block.shape[dim] - width, None, axis...  61.3 us
    dot_general x16, matrix products, add_block(): jnp.dot(piece_values, one_hot, preferred_element_type=jnp.float32)  42.7 us
    unnamed x79, local copies, waits for them, and re-layouts  40.2 us
    another operation x30, other arithmetic, spd_solve(): factor = jnp.linalg.cholesky(matrix)  36.1 us
    another operation x20, other arithmetic, spd_solve(): return jax.scipy.linalg.cho_solve((factor, True), right)  32.2 us
    scatter x1, local copies, waits for them, and re-layouts, body(): jnp.zeros((currents.shape[0], slots_all), jnp.bfloat16).at[:, slot_index]  23.7 us
  transfers between devices with their start and end apart: 36, of which 11 were waited for; matrix products, arithmetic and copies ran while one was open for 10% of the time, Pallas kernels for 0%

commit v1 on v0

--- a/solution.py
+++ b/solution.py
@@ -118,7 +118,7 @@
         iterate = voltage
         residual = rhs - apply_grid(iterate)
         direction = residual
-        norm_gram = lax.psum(gram(residual, residual), ("gx", "gy"))
+        norm_gram = lax.psum(lax.psum(gram(residual, residual), "gy"), "gx")
         for sweep in range(ITERS):
             image = apply_grid(direction)
             curve_gram, cross_gram, image_gram = lax.psum(

time: 657 us -> 727 us (1.11)
  blocking collectives: 266 us -> 337 us
    psum x4 -> x6, blocking collectives: 174 us -> 253 us  [body(): lax.psum((gram(direction, image), gram(residual, image), gram(image, imag...]
    psum x2 -> x4, blocking collectives: 91.3 us -> 84 us  [body(): norm_gram = lax.psum(lax.psum(gram(residual, residual), 'gy'), 'gx')]
  transfers between devices with their start and end apart: 36 -> 36, of which waited for: 11 -> 9; matrix products, arithmetic and copies ran while one was open for 10% -> 10% of each run, Pallas kernels for 0% -> 0%
where the time goes in v1:
time: 727 us; the launch traced here: 717 us
  blocking collectives  337 us (46%)
  local copies, waits for them, and re-layouts  107 us (15%)
  starting transfers between devices  104 us (14%)
  other arithmetic  96 us (13%)
  matrix products  68.3 us (9%)
    psum x6, blocking collectives, body(): lax.psum((gram(direction, image), gram(residual, image), gram(image, imag...  253 us
    psum x4, blocking collectives, body(): norm_gram = lax.psum(lax.psum(gram(residual, residual), 'gy'), 'gx')  84 us
    ppermute x16, starting transfers between devices, with_halo(): lax.ppermute(lax.slice_in_dim(block, block.shape[dim] - width, None, axis...  61 us
    dot_general x16, matrix products, add_block(): jnp.dot(piece_values, one_hot, preferred_element_type=jnp.float32)  42.6 us
    unnamed x79, local copies, waits for them, and re-layouts  39.6 us
    another operation x30, other arithmetic, spd_solve(): factor = jnp.linalg.cholesky(matrix)  36.1 us
    another operation x20, other arithmetic, spd_solve(): return jax.scipy.linalg.cho_solve((factor, True), right)  32.1 us
    scatter x1, local copies, waits for them, and re-layouts, body(): jnp.zeros((currents.shape[0], slots_all), jnp.bfloat16).at[:, slot_index]  23.6 us
  transfers between devices with their start and end apart: 36, of which 9 were waited for; matrix products, arithmetic and copies ran while one was open for 10% of the time, Pallas kernels for 0%

profile of v1, /device:TPU:0, one launch (start us, length us, event | category | flops | bytes accessed | tf_op | source)
XLA Modules:
  0.0 717.0 jit_solution(2779249280779818831)
XLA Ops:
  1.6 9.5 %reduce-window.6 = s32[32,64,128]{2,1,0:T(8,128)S(1)} reduce-window(s32[32,64,128]{2,1,0:T(8,128)S(1)} %fusion.11, s32[]{:T(128)} %constant.128.clone.1), window={size=1x1x128 pad=0_0x0_0x127_0}, to_apply=%region_0.0 | reduce-window | flops 33292288 | bytes 2097156 | tf_op jit(solution)/shard_map/reduce-window
  14.9 23.6 %scatter_custom_fusion = bf16[64,16384]{0,1:T(8,128)(2,1)} fusion(s32[8192]{0:T(1024)S(1)} %bitcast.343, bf16[8192,64]{1,0:T(8,128)(2,1)S(1)} %copy.219, bf16[]{:T(256)} %constant.130.clone.1), kind=kCustom, calls=%fused_computation.13 | custom fusion | bytes 2097154 | tf_op jit(solution)/shard_map/scatter | solution.py:84
  38.5 4.8 copy.220
  43.3 7.3 %all-to-all-start = ((bf16[64,32,512]{2,0,1:T(8,128)(2,1)}), bf16[64,32,512]{2,0,1:T(8,128)(2,1)S(1)}, u32[]{:S(2)}, u32[]{:S(2)}) async-start(bf16[64,32,512]{2,0,1:T(8,128)(2,1)} %copy.220), calls=%async_computation | async-start | bytes 4194304 | tf_op jit(solution)/shard_map/all_to_all | solution.py:87
  62.9 31.2 %scatter_custom_fusion.1 = s32[16384]{0:T(1024)} fusion(s32[8192]{0:T(1024)S(1)} %broadcast_select_fusion, s32[8192]{0:T(1024)} %param.26, s32[]{:T(128)} %constant.128.clone.1), kind=kCustom, calls=%fused_computation.270 | custom fusion | bytes 66048
  97.6 7.3 %all-to-all-start.1 = ((s32[1,32,512]{2,0,1:T(1,128)}), s32[1,32,512]{2,0,1:T(1,128)}, u32[]{:S(2)}, u32[]{:S(2)}) async-start(s32[1,32,512]{2,0,1:T(1,128)} %bitcast.344), calls=%async_computation.1 | async-start | bytes 131072 | tf_op jit(solution)/shard_map/all_to_all | solution.py:88
  110.2 4.7 collective-permute-start.5
  119.0 53.6 %while.16 = (s32[]{:T(128)}, f32[64,1024]{1,0:T(8,128)}, bf16[64,16384]{1,0:T(8,128)(2,1)}, s32[1,16384]{1,0:T(1,128)}, s32[]{:T(128)}, /*index=5*/s32[]{:T(128)}, s32[]{:T(128)}, s32[]{:T(128)}) while((s32[]{:T(128)}, f32[64,1024]{1,0:T(8,128)}, bf16[64,16384]{1,0:T(8,128)(2,1)}, s32[1,16384]{1,0:T(1,128)}, s32[]{:T(128)}, ...), condition=%wide.region_6.7_spmd.clone, body=%wide.region_5.6_spmd.clone.sunk | while | flops 135397376 | bytes 667797 | solution.py:100
  181.2 19.7 %psum.119 = f32[32,32]{0,1:T(8,128)S(1)} all-reduce(f32[32,32]{0,1:T(8,128)S(1)} %convolution_bitcast_fusion.18), channel_id=1, replica_groups=mesh['gx'=8,'gy'=4] {'gy'}, use_global_device_ids=true, to_apply=%region_10.12 | all-reduce | flops 1024 | bytes 8192 | tf_op jit(solution)/shard_map/psum | solution.py:121
  200.9 22.3 %psum.120 = f32[32,32]{0,1:T(8,128)S(1)} all-reduce(f32[32,32]{0,1:T(8,128)S(1)} %psum.119), channel_id=1, replica_groups=mesh['gx'=8,'gy'=4] {'gx'}, use_global_device_ids=true, to_apply=%region_11.13 | all-reduce | flops 1024 | bytes 8192 | tf_op jit(solution)/shard_map/psum | solution.py:121
  229.7 4.5 collective-permute-start.9
  241.3 37.9 %all-reduce.21 = (f32[32,32]{0,1:T(8,128)S(1)}, f32[32,32]{1,0:T(8,128)S(1)}) all-reduce(f32[32,32]{0,1:T(8,128)S(1)} %convolution_bitcast_fusion.19, f32[32,32]{1,0:T(8,128)S(1)} %convolution_bitcast_fusion.17), channel_id=1, replica_groups=mesh['gx'=8,'gy'=4] {'gx','gy'}, use_global_device_ids=true, to_apply=%region_7.8 | all-reduce | flops 2048 | bytes 16384 | tf_op jit(solution)/shard_map/psum | solution.py:124
  302.1 4.8 collective-permute-start.13
  314.7 43.8 %all-reduce.20 = (f32[32,32]{0,1:T(8,128)S(1)}, f32[32,32]{1,0:T(8,128)S(1)}, f32[32,32]{1,0:T(8,128)S(1)}) all-reduce(f32[32,32]{0,1:T(8,128)S(1)} %convolution_bitcast_fusion.15, f32[32,32]{1,0:T(8,128)S(1)} %convolution_bitcast_fusion.13, f32[32,32]{1,0:T(8,128)S(1)} %convolution_bitcast_fusion.14), channel_id=1, replica_groups=mesh['gx'=8,'gy'=4] {'gx','gy'}, use_global_device_ids=true, to_apply=%region_13.16 | all-reduce | flops 3072 | bytes 24576 | tf_op jit(solution)/shard_map/psum | solution.py:124
  376.5 4.5 collective-permute-start.17
  383.9 43.8 %psum.125 = f32[32,32]{0,1:T(8,128)S(1)} all-reduce(f32[32,32]{0,1:T(8,128)S(1)} %convolution_bitcast_fusion.11), channel_id=1, replica_groups=mesh['gx'=8,'gy'=4] {'gx','gy'}, use_global_device_ids=true, to_apply=%region_16.19 | all-reduce | flops 1024 | bytes 8192 | tf_op jit(solution)/shard_map/psum | solution.py:124
  444.3 5.0 collective-permute-start.21
  458.4 17.4 %psum.127 = f32[32,32]{0,1:T(8,128)S(1)} all-reduce(f32[32,32]{0,1:T(8,128)S(1)} %convolution_bitcast_fusion.8), channel_id=1, replica_groups=mesh['gx'=8,'gy'=4] {'gy'}, use_global_device_ids=true, to_apply=%region_18.21 | all-reduce | flops 1024 | bytes 8192 | tf_op jit(solution)/shard_map/psum | solution.py:121
  475.9 24.6 %psum.128 = f32[32,32]{0,1:T(8,128)S(1)} all-reduce(f32[32,32]{0,1:T(8,128)S(1)} %psum.127), channel_id=1, replica_groups=mesh['gx'=8,'gy'=4] {'gx'}, use_global_device_ids=true, to_apply=%region_19.22 | all-reduce | flops 1024 | bytes 8192 | tf_op jit(solution)/shard_map/psum | solution.py:121
  506.4 4.5 collective-permute-start.25
  517.6 39.0 %all-reduce.19 = (f32[32,32]{0,1:T(8,128)S(1)}, f32[32,32]{1,0:T(8,128)S(1)}) all-reduce(f32[32,32]{0,1:T(8,128)S(1)} %convolution_bitcast_fusion.9, f32[32,32]{1,0:T(8,128)S(1)} %convolution_bitcast_fusion.7), channel_id=1, replica_groups=mesh['gx'=8,'gy'=4] {'gx','gy'}, use_global_device_ids=true, to_apply=%region_17.20 | all-reduce | flops 2048 | bytes 16384 | tf_op jit(solution)/shard_map/psum | solution.py:124
  578.9 4.7 collective-permute-start.29
  591.3 44.4 %all-reduce.18 = (f32[32,32]{0,1:T(8,128)S(1)}, f32[32,32]{1,0:T(8,128)S(1)}, f32[32,32]{1,0:T(8,128)S(1)}) all-reduce(f32[32,32]{0,1:T(8,128)S(1)} %convolution_bitcast_fusion.5, f32[32,32]{1,0:T(8,128)S(1)} %convolution_bitcast_fusion.3, f32[32,32]{1,0:T(8,128)S(1)} %convolution_bitcast_fusion.4), channel_id=1, replica_groups=mesh['gx'=8,'gy'=4] {'gx','gy'}, use_global_device_ids=true, to_apply=%region_21.24 | all-reduce | flops 3072 | bytes 24576 | tf_op jit(solution)/shard_map/psum | solution.py:124
  662.4 43.8 %psum.133 = f32[32,32]{0,1:T(8,128)S(1)} all-reduce(f32[32,32]{0,1:T(8,128)S(1)} %convolution_bitcast_fusion.1), channel_id=1, replica_groups=mesh['gx'=8,'gy'=4] {'gx','gy'}, use_global_device_ids=true, to_apply=%region_24.27 | all-reduce | flops 1024 | bytes 8192 | tf_op jit(solution)/shard_map/psum | solution.py:124
  (402 shorter events, 261.3 us)
Async XLA Ops:
  43.3 54.2 %all-to-all-start = ((bf16[64,32,512]{2,0,1:T(8,128)(2,1)}), bf16[64,32,512]{2,0,1:T(8,128)(2,1)S(1)}, u32[]{:S(2)}, u32[]{:S(2)}) async-start(bf16[64,32,512]{2,0,1:T(8,128)(2,1)} %copy.220), calls=%async_computation | async-start | bytes 4194304 | tf_op jit(solution)/shard_map/all_to_all | solution.py:87
  51.7 43.5 %collective-permute-start.2 = (f32[32,4,1,128]{3,0,2,1:T(8,128)S(1)}, f32[32,4,1,128]{3,0,2,1:T(8,128)S(1)}, u32[]{:S(2)}, u32[]{:S(2)}) collective-permute-start(f32[32,4,1,128]{3,0,2,1:T(8,128)S(1)} %get-tuple-element.213), channel_id=1, source_target_pairs={{0,4},{4,8},{8,12},{12,16},{16,20},{20,24},{24,28},{1,5},{5,9},{9,... | collective-permute-start | bytes 196616 | tf_op jit(solution)/shard_map/ppermute | solution.py:14
  53.8 43.6 %collective-permute-start = (f32[32,4,1,128]{3,0,2,1:T(8,128)}, f32[32,4,1,128]{3,0,2,1:T(8,128)S(1)}, u32[]{:S(2)}, u32[]{:S(2)}) collective-permute-start(f32[32,4,1,128]{3,0,2,1:T(8,128)} %get-tuple-element.212), channel_id=1, source_target_pairs={{4,0},{8,4},{12,8},{16,12},{20,16},{24,20},{28,24},{5,1},{9,5},{13... | collective-permute-start | bytes 196616 | tf_op jit(solution)/shard_map/ppermute | solution.py:17
  55.2 39.9 %collective-permute-start.4 = (f32[4,8,1]{2,1,0:T(8,128)S(1)}, f32[4,8,1]{2,1,0:T(8,128)S(1)}, u32[]{:S(2)}, u32[]{:S(2)}) collective-permute-start(f32[4,8,1]{2,1,0:T(8,128)S(1)} %slice.379), channel_id=1, source_target_pairs={{0,1},{1,2},{2,3},{4,5},{5,6},{6,7},{8,9},{9,10},{10,11},{12,13},{... | collective-permute-start | bytes 392 | tf_op jit(solution)/shard_map/ppermute | solution.py:25
  58.8 56.2 %collective-permute-start.1 = (f32[4,1,128]{2,1,0:T(1,128)S(1)}, f32[4,1,128]{2,1,0:T(1,128)S(1)}, u32[]{:S(2)}, u32[]{:S(2)}) collective-permute-start(f32[4,1,128]{2,1,0:T(1,128)S(1)} %slice.373), channel_id=1, source_target_pairs={{0,4},{4,8},{8,12},{12,16},{16,20},{20,24},{24,28},{1,5},{5,9},{9,... | collective-permute-start | bytes 6152 | tf_op jit(solution)/shard_map/ppermute | solution.py:25
  97.6 21.4 %all-to-all-start.1 = ((s32[1,32,512]{2,0,1:T(1,128)}), s32[1,32,512]{2,0,1:T(1,128)}, u32[]{:S(2)}, u32[]{:S(2)}) async-start(s32[1,32,512]{2,0,1:T(1,128)} %bitcast.344), calls=%async_computation.1 | async-start | bytes 131072 | tf_op jit(solution)/shard_map/all_to_all | solution.py:88
  107.5 7.4 %collective-permute-start.3 = (f32[32,4,10,1]{0,1,3,2:T(4,128)S(1)}, f32[32,4,10,1]{0,1,3,2:T(4,128)S(1)}, u32[]{:S(2)}, u32[]{:S(2)}) collective-permute-start(f32[32,4,10,1]{0,1,3,2:T(4,128)S(1)} %copy.230), channel_id=1, source_target_pairs={{1,0},{2,1},{3,2},{5,4},{6,5},{7,6},{9,8},{10,9},{11,10},{13,12},{... | collective-permute-start | bytes 15368 | tf_op jit(solution)/shard_map/ppermute | solution.py:17
  110.2 6.0 collective-permute-start.5
  176.8 50.1 %collective-permute-start.6 = (f32[32,4,1,128]{3,0,2,1:T(8,128)S(1)}, f32[32,4,1,128]{3,0,2,1:T(8,128)S(1)}, u32[]{:S(2)}, u32[]{:S(2)}) collective-permute-start(f32[32,4,1,128]{3,0,2,1:T(8,128)S(1)} %get-tuple-element.209), channel_id=1, source_target_pairs={{4,0},{8,4},{12,8},{16,12},{20,16},{24,20},{28,24},{5,1},{9,5},{13... | collective-permute-start | bytes 196616 | tf_op jit(solution)/shard_map/ppermute | solution.py:17
  178.1 48.8 %collective-permute-start.7 = (f32[32,4,1,128]{3,0,2,1:T(8,128)S(1)}, f32[32,4,1,128]{3,0,2,1:T(8,128)S(1)}, u32[]{:S(2)}, u32[]{:S(2)}) collective-permute-start(f32[32,4,1,128]{3,0,2,1:T(8,128)S(1)} %get-tuple-element.208), channel_id=1, source_target_pairs={{0,4},{4,8},{8,12},{12,16},{16,20},{20,24},{24,28},{1,5},{5,9},{9,... | collective-permute-start | bytes 196616 | tf_op jit(solution)/shard_map/ppermute | solution.py:14
  228.1 9.9 %collective-permute-start.8 = (f32[32,4,10,1]{0,1,3,2:T(4,128)S(1)}, f32[32,4,10,1]{0,1,3,2:T(4,128)S(1)}, u32[]{:S(2)}, u32[]{:S(2)}) collective-permute-start(f32[32,4,10,1]{0,1,3,2:T(4,128)S(1)} %copy.240), channel_id=1, source_target_pairs={{1,0},{2,1},{3,2},{5,4},{6,5},{7,6},{9,8},{10,9},{11,10},{13,12},{... | collective-permute-start | bytes 15368 | tf_op jit(solution)/shard_map/ppermute | solution.py:17
  229.7 8.7 %collective-permute-start.9 = (f32[32,4,10,1]{0,1,3,2:T(4,128)S(1)}, f32[32,4,10,1]{0,1,3,2:T(4,128)S(1)}, u32[]{:S(2)}, u32[]{:S(2)}) collective-permute-start(f32[32,4,10,1]{0,1,3,2:T(4,128)S(1)} %copy.242), channel_id=1, source_target_pairs={{0,1},{1,2},{2,3},{4,5},{5,6},{6,7},{8,9},{9,10},{10,11},{12,13},{... | collective-permute-start | bytes 15368 | tf_op jit(solution)/shard_map/ppermute | solution.py:14
  300.5 10.1 %collective-permute-start.12 = (f32[32,4,10,1]{0,1,3,2:T(4,128)S(1)}, f32[32,4,10,1]{0,1,3,2:T(4,128)S(1)}, u32[]{:S(2)}, u32[]{:S(2)}) collective-permute-start(f32[32,4,10,1]{0,1,3,2:T(4,128)S(1)} %copy.254), channel_id=1, source_target_pairs={{1,0},{2,1},{3,2},{5,4},{6,5},{7,6},{9,8},{10,9},{11,10},{13,12},{... | collective-permute-start | bytes 15368 | tf_op jit(solution)/shard_map/ppermute | solution.py:17
  302.1 8.8 %collective-permute-start.13 = (f32[32,4,10,1]{0,1,3,2:T(4,128)S(1)}, f32[32,4,10,1]{0,1,3,2:T(4,128)S(1)}, u32[]{:S(2)}, u32[]{:S(2)}) collective-permute-start(f32[32,4,10,1]{0,1,3,2:T(4,128)S(1)} %copy.256), channel_id=1, source_target_pairs={{0,1},{1,2},{2,3},{4,5},{5,6},{6,7},{8,9},{9,10},{10,11},{12,13},{... | collective-permute-start | bytes 15368 | tf_op jit(solution)/shard_map/ppermute | solution.py:14
  374.9 6.3 collective-permute-start.16
  442.7 6.6 collective-permute-start.20
  444.3 6.0 collective-permute-start.21
  453.8 50.4 %collective-permute-start.22 = (f32[32,4,1,128]{3,0,2,1:T(8,128)S(1)}, f32[32,4,1,128]{3,0,2,1:T(8,128)S(1)}, u32[]{:S(2)}, u32[]{:S(2)}) collective-permute-start(f32[32,4,1,128]{3,0,2,1:T(8,128)S(1)} %get-tuple-element.193), channel_id=1, source_target_pairs={{4,0},{8,4},{12,8},{16,12},{20,16},{24,20},{28,24},{5,1},{9,5},{13... | collective-permute-start | bytes 196616 | tf_op jit(solution)/shard_map/ppermute | solution.py:17
  455.1 49.1 %collective-permute-start.23 = (f32[32,4,1,128]{3,0,2,1:T(8,128)S(1)}, f32[32,4,1,128]{3,0,2,1:T(8,128)S(1)}, u32[]{:S(2)}, u32[]{:S(2)}) collective-permute-start(f32[32,4,1,128]{3,0,2,1:T(8,128)S(1)} %get-tuple-element.192), channel_id=1, source_target_pairs={{0,4},{4,8},{8,12},{12,16},{16,20},{20,24},{24,28},{1,5},{5,9},{9,... | collective-permute-start | bytes 196616 | tf_op jit(solution)/shard_map/ppermute | solution.py:14
  504.8 9.3 %collective-permute-start.24 = (f32[32,4,10,1]{0,1,3,2:T(4,128)S(1)}, f32[32,4,10,1]{0,1,3,2:T(4,128)S(1)}, u32[]{:S(2)}, u32[]{:S(2)}) collective-permute-start(f32[32,4,10,1]{0,1,3,2:T(4,128)S(1)} %copy.278), channel_id=1, source_target_pairs={{1,0},{2,1},{3,2},{5,4},{6,5},{7,6},{9,8},{10,9},{11,10},{13,12},{... | collective-permute-start | bytes 15368 | tf_op jit(solution)/shard_map/ppermute | solution.py:17
  506.4 8.0 %collective-permute-start.25 = (f32[32,4,10,1]{0,1,3,2:T(4,128)S(1)}, f32[32,4,10,1]{0,1,3,2:T(4,128)S(1)}, u32[]{:S(2)}, u32[]{:S(2)}) collective-permute-start(f32[32,4,10,1]{0,1,3,2:T(4,128)S(1)} %copy.280), channel_id=1, source_target_pairs={{0,1},{1,2},{2,3},{4,5},{5,6},{6,7},{8,9},{9,10},{10,11},{12,13},{... | collective-permute-start | bytes 15368 | tf_op jit(solution)/shard_map/ppermute | solution.py:14
  577.3 10.0 %collective-permute-start.28 = (f32[32,4,10,1]{0,1,3,2:T(4,128)S(1)}, f32[32,4,10,1]{0,1,3,2:T(4,128)S(1)}, u32[]{:S(2)}, u32[]{:S(2)}) collective-permute-start(f32[32,4,10,1]{0,1,3,2:T(4,128)S(1)} %copy.291), channel_id=1, source_target_pairs={{1,0},{2,1},{3,2},{5,4},{6,5},{7,6},{9,8},{10,9},{11,10},{13,12},{... | collective-permute-start | bytes 15368 | tf_op jit(solution)/shard_map/ppermute | solution.py:17
  578.9 8.7 %collective-permute-start.29 = (f32[32,4,10,1]{0,1,3,2:T(4,128)S(1)}, f32[32,4,10,1]{0,1,3,2:T(4,128)S(1)}, u32[]{:S(2)}, u32[]{:S(2)}) collective-permute-start(f32[32,4,10,1]{0,1,3,2:T(4,128)S(1)} %copy.293), channel_id=1, source_target_pairs={{0,1},{1,2},{2,3},{4,5},{5,6},{6,7},{8,9},{9,10},{10,11},{12,13},{... | collective-permute-start | bytes 15368 | tf_op jit(solution)/shard_map/ppermute | solution.py:14
  652.1 7.1 collective-permute-start.32
  (49 other events, 732.7 us)
